TPU v7x, 32 devices: a whole 2x2x4 slice. The times are simulated.
32 devices in a mesh: dp: 4 (over y, x), expert: 8 (over z, core).
Axes of the slice: x: 2, y: 2, z: 4, core: 2. Of those that a mesh axis runs over, the one named last changes fastest.
Arguments:
- tokens: bfloat16 [4096, 4096], P(('dp', 'expert')), may hold values from -6 to 6
- gate_proj: bfloat16 [8, 768, 4096], P('expert', 'dp'), may hold values from -0.09375 to 0.09375
- up_proj: bfloat16 [8, 768, 4096], P('expert', 'dp'), may hold values from -0.09375 to 0.09375
- down_proj: bfloat16 [8, 768, 4096], P('expert', 'dp'), may hold values from -0.21875 to 0.21875
- route_ids: int32 [4096, 2], P(('dp', 'expert')), may hold values from 0 to 7, as said below
- route_slots: int32 [4096, 2], P(('dp', 'expert')), may hold values from 0 to 95, as said below
- route_gates: float32 [4096, 2], P(('dp', 'expert')), may hold values from 0.1 to 1
- image_shard: int32 [4, 8], P(None, 'expert'), may hold values from 0 to 3, as said below
- norm_gain: float32 [4096], replicated, may hold values from 0.5 to 1.5
- key_proj: bfloat16 [4096, 1024], P('dp'), may hold values from -0.09375 to 0.09375
Outputs:
- student_rows: bfloat16 [4096, 4096], P(('dp', 'expert'))
- keys: bfloat16 [4096, 1024], P(('dp', 'expert'))
Inputs may be any that keep to these rules, and one draw needn't show every extreme that they name: `route_ids`: within the rows of one device a token names 2 different experts and no expert is named more than 2 * 48 times; on every device some expert is named exactly 2 * 48 times. `route_slots`: within the rows of one device the mentions of one expert carry the numbers 0 up to their count minus one, each once; one expert has 48 retained mentions from every device. `image_shard`: for each e, of the 4 image tiles of column e exactly 1 name each shard.
All inputs are finite; a program needn't handle non-finite values.
Results may differ from a plain program's by a relative error of at most 0.007.
Values may be sent and summed in bfloat16 or wider, within the bound.
A program may use at most 128 MiB of HBM per device.

v0:
```python
import functools

import jax
import jax.numpy as jnp
from jax import lax
from jax.experimental import pallas as pl
from jax.experimental.pallas import tpu as pltpu
from jax.sharding import PartitionSpec as P

IMG_TOK = 128


def normalize(values, norm_gain):
    wide = values.astype(jnp.float32)
    mean_square = jnp.mean(wide * wide, axis=-1, keepdims=True)
    return (wide * lax.rsqrt(mean_square + 1e-05) * norm_gain).astype(jnp.bfloat16)


def activate(incoming, gate_rows, up_rows):
    dims = (((1,), (1,)), ((), ()))
    gate_act = lax.dot_general(incoming, gate_rows, dims, preferred_element_type=jnp.float32)
    up_act = lax.dot_general(incoming, up_rows, dims, preferred_element_type=jnp.float32)
    return (jax.nn.silu(gate_act) * up_act).astype(jnp.bfloat16)


CHUNKS = 4
PIECES = 2
GROUP = 16
MESH = pl.DeviceIdType.MESH


def fused_kernel(
    n_expert,
    capacity,
    ids_ref,
    slots_ref,
    gates_ref,
    shard_ref,
    gain_ref,
    tokens_ref,
    gate_ref,
    up_ref,
    down_ref,
    key_ref,
    student_ref,
    keys_ref,
    gate_buf,
    up_buf,
    down_buf,
    key_buf,
    outgoing,
    incoming,
    produced,
    returned,
    tiles,
    passed,
    far,
    tok_half,
    hidden,
    gained,
    mixing,
    acc_keys,
    acc_gate,
    acc_up,
    squares,
    send_sem,
    recv_sem,
    spare_send,
    spare_recv,
    local_sem,
):
    d = lax.axis_index("dp")
    e = lax.axis_index("expert")
    dx = d + 1 - 2 * (d % 2)
    dy = (d + 2) % 4
    dd = (dx + 2) % 4
    core = e % 2
    sibling = e + 1 - 2 * core
    w = dx + core * (dy - dx)
    t = dy + core * (dx - dy)
    tok_dev, width = tokens_ref.shape
    units = gate_ref.shape[1]
    half = width // 2
    quarter_width = width // 4
    chunk = half // CHUNKS
    per_quarter = CHUNKS // 2
    key_rows, key_width = key_ref.shape
    key_half = key_rows // 2
    piece = key_half // PIECES
    half_piece = piece // 2
    slots = n_expert * capacity
    groups = capacity // GROUP
    block = n_expert * GROUP
    counts = {"remote": 0, "local": 0}
    sent = []

    def send(source, target, where):
        index = counts["remote"]
        counts["remote"] += 1
        copy = pltpu.make_async_remote_copy(
            src_ref=source,
            dst_ref=target,
            send_sem=send_sem.at[index],
            recv_sem=recv_sem.at[index],
            device_id=where,
            device_id_type=MESH,
        )
        copy.start()
        sent.append(copy)
        return copy

    def local(source, target):
        index = counts["local"]
        counts["local"] += 1
        copy = pltpu.make_async_copy(source, target, local_sem.at[index])
        copy.start()
        return copy

    to_x, to_y, to_sibling = {"dp": dx}, {"dp": dy}, {"expert": sibling}
    to_w, to_t, to_d = {"dp": w}, {"dp": t}, {"dp": dd}
    hops = range(1, n_expert)
    peers = {k: lax.rem(e + k, n_expert) for k in hops}
    senders = {k: lax.rem(e + n_expert - k, n_expert) for k in hops}

    def quarter_of(owner, p):
        return (owner // 2) * 2 + p

    def unit_rows(owner):
        place = owner % 2 + core * (owner // 2 - owner % 2)
        return pl.ds(pl.multiple_of(place * units, units), units)

    def quarter_cols(owner, p):
        return pl.ds(pl.multiple_of(quarter_of(owner, p) * quarter_width, quarter_width), quarter_width)

    def chunk_cols(owner, c):
        first = quarter_of(owner, c // per_quarter) * quarter_width + (c % per_quarter) * chunk
        return pl.ds(pl.multiple_of(first, chunk), chunk)

    def group_rows(g, who):
        return pl.ds(pl.multiple_of(g * block + who * GROUP, GROUP), GROUP)

    def incoming_rows(g, s, who):
        return pl.ds(pl.multiple_of((g * 2 + s) * block + who * GROUP, GROUP), GROUP)

    barrier = pltpu.get_barrier_semaphore()
    for where in [to_x, to_y, to_d] + [{"expert": peers[k]} for k in hops]:
        pl.semaphore_signal(barrier, inc=1, device_id=where, device_id_type=MESH)
    pl.semaphore_wait(barrier, n_expert + 2)

    mine = unit_rows(d)
    gate_w = send(gate_ref.at[0], gate_buf.at[mine, :], to_w)
    up_w = send(up_ref.at[0], up_buf.at[mine, :], to_w)
    down_x, down_y, down_f, own_down = [], [], [], []
    for p in range(2):
        cols = pl.ds(p * quarter_width, quarter_width)
        down_y.append(
            send(down_ref.at[0, :, quarter_cols(dy, p)], down_buf.at[1 - core, mine, cols], to_y)
        )
    own_gate = local(gate_ref.at[0], gate_buf.at[mine, :])
    own_up = local(up_ref.at[0], up_buf.at[mine, :])
    for p in range(2):
        cols = pl.ds(p * quarter_width, quarter_width)
        down_x.append(send(down_ref.at[0, :, quarter_cols(d, p)], down_buf.at[core, mine, cols], to_x))
        own_down.append(local(down_ref.at[0, :, quarter_cols(d, p)], down_buf.at[0, mine, cols]))
    own_key = local(key_ref, key_buf.at[d])

    step = 512
    grid = lax.broadcasted_iota(jnp.int32, (slots, tok_dev), 0)
    mix = jnp.zeros((slots, tok_dev), jnp.float32)
    named = jnp.zeros((slots, tok_dev), jnp.float32)
    for k in range(ids_ref.shape[0]):
        queue = slots_ref[k : k + 1, :]
        place = lax.div(queue, GROUP) * block + ids_ref[k : k + 1, :] * GROUP + lax.rem(queue, GROUP)
        cell = jnp.where(queue < capacity, place, slots)
        hit = grid == cell
        mix += jnp.where(hit, gates_ref[k : k + 1, :], 0.0)
        named += jnp.where(hit, 1.0, 0.0)
    spread = named.astype(jnp.bfloat16)

    dispatched, forwarded = [], []
    for g in range(groups):
        chosen = spread[g * block : (g + 1) * block, :]

        def fill(i, carry):
            cols = pl.ds(pl.multiple_of(i * step, step), step)
            rows = jnp.dot(chosen, tokens_ref[:, cols], preferred_element_type=jnp.float32)
            outgoing[pl.ds(g * block, block), cols] = rows.astype(jnp.bfloat16)
            return carry

        lax.fori_loop(0, width // step, fill, 0)
        dispatched.append(
            {
                k: send(
                    outgoing.at[group_rows(g, peers[k]), :],
                    incoming.at[incoming_rows(g, 0, e), :],
                    {"expert": peers[k]},
                )
                for k in hops
            }
        )
        forwarded.append(
            [send(outgoing.at[group_rows(g, e), :], incoming.at[incoming_rows(g, 1, e), :], to_t)]
        )
        incoming[incoming_rows(g, 0, e), :] = outgoing[group_rows(g, e), :]

    turned = mix.T
    mix_hi = turned.astype(jnp.bfloat16)
    mixing[0, 0] = mix_hi
    mixing[0, 1] = (turned - mix_hi.astype(jnp.float32)).astype(jnp.bfloat16)

    def forward(g):
        for k in hops:
            dispatched[g][k].wait_recv()
            forwarded[g].append(
                send(
                    incoming.at[incoming_rows(g, 0, senders[k]), :],
                    incoming.at[incoming_rows(g, 1, senders[k]), :],
                    to_t,
                )
            )

    dims = (((1,), (1,)), ((), ()))
    deep = 1024
    handed, spares = [], []

    def activate(g):
        for copy in forwarded[g]:
            copy.wait_recv()
        here = pl.ds(g * 2 * block, 2 * block)
        acc_gate[...] = jnp.zeros_like(acc_gate)
        acc_up[...] = jnp.zeros_like(acc_up)

        def add(i, carry):
            cols = pl.ds(pl.multiple_of(i * deep, deep), deep)
            rows = incoming[here, cols]
            acc_gate[...] += lax.dot_general(
                rows, gate_buf[:, cols], dims, preferred_element_type=jnp.float32
            )
            acc_up[...] += lax.dot_general(
                rows, up_buf[:, cols], dims, preferred_element_type=jnp.float32
            )
            return carry

        lax.fori_loop(0, width // deep, add, 0)
        gate_act = acc_gate[...]
        act = (gate_act / (1.0 + jnp.exp(-gate_act)) * acc_up[...]).astype(jnp.bfloat16)
        at = pl.ds(g * block, block)
        hidden[0, at, :] = act[:block]
        hidden[1 + 3 * core, at, :] = act[block:]
        handed.append(
            [
                send(hidden.at[0, at, :], hidden.at[3 - 2 * core, at, :], to_y),
                send(hidden.at[1 + 3 * core, at, :], hidden.at[2, at, :], to_t),
            ]
        )
        spare = pltpu.make_async_remote_copy(
            src_ref=hidden.at[4, at, :],
            dst_ref=hidden.at[3, at, :],
            send_sem=spare_send.at[g],
            recv_sem=spare_recv.at[g],
            device_id=to_d,
            device_id_type=MESH,
        )
        spares.append(spare)

        @pl.when(core == 1)
        def _():
            spare.start()

    hands = []

    def give(g, cols):
        for s in range(2):
            returned[s, group_rows(g, e), cols] = produced[g * 2 + s, pl.ds(pl.multiple_of(e * GROUP, GROUP), GROUP), cols]
        return [
            send(
                produced.at[pl.ds(g * 2, 2), pl.ds(pl.multiple_of(peers[k] * GROUP, GROUP), GROUP), cols],
                returned.at[:, group_rows(g, e), cols],
                {"expert": peers[k]},
            )
            for k in hops
        ]

    def project(g, first, count):
        here = pl.ds(g * block, block)

        def one(i, carry):
            at = pl.ds(pl.multiple_of(i * chunk, chunk), chunk)
            total = jnp.zeros((2 * block, chunk), jnp.float32)
            for pair in range(2):
                acts = hidden[pl.ds(2 * pair, 2), here, :].reshape(2 * block, 2 * units)
                total += jnp.dot(acts, down_buf[pair, :, at], preferred_element_type=jnp.float32)
            rows = total.astype(jnp.bfloat16)
            produced[g * 2, :, at] = rows[:block]
            produced[g * 2 + 1, :, at] = rows[block:]
            return carry

        lax.fori_loop(first, first + count, one, 0)

    def key_rows_at(owner, p, start=0, size=piece):
        first = (owner % 2) * key_half + p * piece + start
        return pl.ds(pl.multiple_of(first, half_piece), size)

    key_first, key_second, key_shared = [], [], []

    def key_own(p):
        rows = key_rows_at(e, p)
        part = key_ref.at[rows, :]
        place = key_buf.at[d, rows, :]
        key_first.append((send(part, place, to_x), send(part, place, to_y)))

    def pass_key(owner, rows, where):
        part = key_buf.at[owner, rows, :]
        return send(part, part, where)

    def key_share(owner, rows):
        key_shared.append(pass_key(owner, rows, to_sibling))

    def key_middle(p):
        key_x, key_y = key_first[p]
        rows = key_rows_at(e, p)
        key_y.wait_recv()
        d0 = pass_key(dy, key_rows_at(e, p, 0, half_piece), to_x)
        key_x.wait_recv()
        d1 = pass_key(dx, key_rows_at(e, p, half_piece, half_piece), to_y)
        key_second.append((d0, d1))
        key_share(dy, rows)
        key_share(dx, rows)

    def key_diagonal(p):
        d0, d1 = key_second[p]
        d0.wait_recv()
        key_share(dd, key_rows_at(e, p, 0, half_piece))
        d1.wait_recv()
        key_share(dd, key_rows_at(e, p, half_piece, half_piece))

    def collect(g):
        for copy in handed[g]:
            copy.wait_recv()

        @pl.when(core == 1)
        def _():
            spares[g].wait_recv()

    acc_keys[...] = jnp.zeros_like(acc_keys)
    squares[...] = jnp.zeros_like(squares)
    owners = (d, dy, dx, dd)
    tile_w, tile_t = [], []

    def flag(owner, shard):
        return jnp.where(shard_ref[owner] == shard, 1.0, 0.0)

    def combine(c):
        for copy in hands[groups - 1 + c]:
            copy.wait_recv()
        cols = pl.ds(c * chunk, chunk)
        for s in range(2):
            rows = returned[s, :, cols]
            branch = jnp.dot(mixing[s, 0], rows, preferred_element_type=jnp.float32)
            branch += jnp.dot(mixing[s, 1], rows, preferred_element_type=jnp.float32)
            base = tokens_ref[:, chunk_cols(d, c)] if s == 0 else tok_half[:, cols]
            tiles[s, :, cols] = (base.astype(jnp.float32) + branch).astype(jnp.bfloat16)
        tile_w.append(send(tiles.at[pl.ds(0, 2), :, cols], tiles.at[pl.ds(2, 2), :, cols], to_x))

    def keep(rows, at):
        student_ref[:, at] = rows.astype(jnp.bfloat16)
        gained[:, at] = (rows * gain_ref[:, at]).astype(jnp.bfloat16)
        squares[...] += jnp.sum(rows * rows, axis=-1, keepdims=True)

    def swap(c):
        tile_w[c].wait_recv()
        cols = pl.ds(c * chunk, chunk)
        stay = jnp.zeros((tok_dev, chunk), jnp.float32)
        leave = jnp.zeros((tok_dev, chunk), jnp.float32)
        for slot in range(4):
            rows = tiles[slot, :, cols].astype(jnp.float32)
            stay += flag(owners[slot], d) * rows
            leave += flag(owners[slot], dy) * rows
        passed[:, cols] = leave.astype(jnp.bfloat16)
        tile_t.append(send(passed.at[:, cols], far.at[:, cols], to_y))
        keep(stay, chunk_cols(d, c))

    def finish(c):
        tile_t[c].wait_recv()
        keep(far[:, pl.ds(c * chunk, chunk)].astype(jnp.float32), chunk_cols(dy, c))

    def keys_of(owner, c):
        q = quarter_of(owner, c // per_quarter)
        acc_keys[...] += jnp.dot(
            gained[:, chunk_cols(owner, c)],
            key_buf[q, pl.ds((c % per_quarter) * chunk, chunk), :],
            preferred_element_type=jnp.float32,
        )

    forward(0)
    for p in range(2):
        cols = pl.ds(p * quarter_width, quarter_width)
        down_y[p].wait_recv()
        part = down_buf.at[1 - core, unit_rows(dy), cols]
        down_f.append(send(part, down_buf.at[1, unit_rows(dy), cols], to_x))
    forward(1)
    for copy in (own_gate, own_up):
        copy.wait()
    for copy in (gate_w, up_w):
        copy.wait_recv()
    activate(0)
    for g in range(1, groups - 1):
        activate(g)
    for g in range(2, groups):
        forward(g)
    others = [send(mixing.at[0], mixing.at[1], to_y)]
    for p in range(2):
        cols = pl.ds(p * quarter_width, quarter_width)
        others.append(send(tokens_ref.at[:, quarter_cols(dy, p)], tok_half.at[:, cols], to_y))
    for copy in own_down:
        copy.wait()
    for copy in down_x + down_f:
        copy.wait_recv()
    every = pl.ds(0, half)
    for g in range(groups):
        if g == 1:
            activate(groups - 1)
            for p in range(PIECES):
                key_own(p)
        collect(g)
        if g < groups - 1:
            project(g, 0, CHUNKS)
            hands.append(give(g, every))
        else:
            for c in range(CHUNKS):
                project(g, c, 1)
                hands.append(give(g, pl.ds(c * chunk, chunk)))
    for p in range(PIECES):
        key_middle(p)
    for p in range(PIECES):
        key_diagonal(p)
    for copy in others:
        copy.wait_recv()
    for g in range(groups - 1):
        for copy in hands[g]:
            copy.wait_recv()
    own_key.wait()
    for c in range(CHUNKS + 2):
        if c < CHUNKS:
            combine(c)
        if 0 <= c - 1 < CHUNKS:
            swap(c - 1)
        if c == 1:
            for copy in key_shared:
                copy.wait_recv()
        if 0 <= c - 1 < CHUNKS:
            keys_of(d, c - 1)
        if 0 <= c - 2 < CHUNKS:
            finish(c - 2)
            keys_of(dy, c - 2)
    scale = lax.rsqrt(squares[...] / width + 1e-05)
    keys_ref[...] = (acc_keys[...] * scale).astype(jnp.bfloat16)
    for copy in sent:
        copy.wait_send()

    @pl.when(core == 1)
    def _():
        for copy in spares:
            copy.wait_send()


def fused(
    tokens,
    gate_proj,
    up_proj,
    down_proj,
    route_ids,
    route_slots,
    route_gates,
    image_shard,
    norm_gain,
    key_proj,
    capacity,
):
    tok_dev, width = tokens.shape
    n_expert = lax.axis_size("expert")
    slots = n_expert * capacity
    groups = capacity // GROUP
    units = gate_proj.shape[1]
    half_width = width // 2
    key_rows, key_width = key_proj.shape
    remote = 8 + 8 * PIECES + (n_expert - 1) * (2 * groups + groups - 1 + CHUNKS) + 3 * groups + 3 + 2 * CHUNKS
    vmem = pl.BlockSpec(memory_space=pltpu.VMEM)
    anywhere = pl.BlockSpec(memory_space=pl.ANY)
    scalars = pl.BlockSpec(memory_space=pltpu.SMEM)
    half = jnp.bfloat16
    return pl.pallas_call(
        functools.partial(fused_kernel, n_expert, capacity),
        out_shape=(
            jax.ShapeDtypeStruct((tok_dev, width), half),
            jax.ShapeDtypeStruct((tok_dev, key_width), half),
        ),
        in_specs=[vmem] * 3 + [scalars] + [vmem] * 2 + [anywhere] * 4,
        out_specs=(vmem, vmem),
        scratch_shapes=[
            pltpu.VMEM((2 * units, width), half),
            pltpu.VMEM((2 * units, width), half),
            pltpu.VMEM((2, 2 * units, half_width), half),
            pltpu.VMEM((4, key_rows, key_width), half),
            pltpu.VMEM((slots, width), half),
            pltpu.VMEM((2 * slots, width), half),
            pltpu.VMEM((2 * groups, n_expert * GROUP, half_width), half),
            pltpu.VMEM((2, slots, half_width), half),
            pltpu.VMEM((4, tok_dev, half_width), half),
            pltpu.VMEM((tok_dev, half_width), half),
            pltpu.VMEM((tok_dev, half_width), half),
            pltpu.VMEM((tok_dev, half_width), half),
            pltpu.VMEM((5, slots, 2 * units), half),
            pltpu.VMEM((tok_dev, width), half),
            pltpu.VMEM((2, 2, tok_dev, slots), half),
            pltpu.VMEM((tok_dev, key_width), jnp.float32),
            pltpu.VMEM((2 * n_expert * GROUP, 2 * units), jnp.float32),
            pltpu.VMEM((2 * n_expert * GROUP, 2 * units), jnp.float32),
            pltpu.VMEM((tok_dev, 1), jnp.float32),
            pltpu.SemaphoreType.DMA((remote,)),
            pltpu.SemaphoreType.DMA((remote,)),
            pltpu.SemaphoreType.DMA((groups,)),
            pltpu.SemaphoreType.DMA((groups,)),
            pltpu.SemaphoreType.DMA((5,)),
        ],
        compiler_params=pltpu.CompilerParams(
            collective_id=0, has_side_effects=True, vmem_limit_bytes=60 * 1024 * 1024
        ),
    )(
        route_ids.T,
        route_slots.T,
        route_gates.T,
        image_shard.reshape(-1),
        norm_gain.reshape(1, -1),
        tokens,
        gate_proj,
        up_proj,
        down_proj,
        key_proj,
    )


def per_device(
    tokens,
    gate_proj,
    up_proj,
    down_proj,
    route_ids,
    route_slots,
    route_gates,
    image_shard,
    norm_gain,
    key_proj,
):
    tok_dev, model_width = tokens.shape
    top_count = route_ids.shape[1]
    experts = gate_proj.shape[0] * lax.axis_size("expert")
    capacity = 3 * tok_dev * top_count // (2 * experts)
    if capacity % 16 == 0 and gate_proj.shape[0] == 1 and lax.axis_size("dp") == 4 and experts % 2 == 0:
        if tok_dev == IMG_TOK and gate_proj.shape[1] % 64 == 0 and key_proj.shape[0] % 512 == 0:
            return fused(
                tokens,
                gate_proj,
                up_proj,
                down_proj,
                route_ids,
                route_slots,
                route_gates,
                image_shard,
                norm_gain,
                key_proj,
                capacity,
            )
    slot_total = experts * capacity
    retained = route_slots < capacity
    slot_cells = jnp.where(retained, route_ids * capacity + route_slots, slot_total).reshape(-1)
    owners = jnp.arange(tok_dev * top_count, dtype=jnp.int32) // top_count
    cell_token = (
        jnp.full((slot_total + 1,), tok_dev, jnp.int32).at[slot_cells].set(owners)[:slot_total]
    )
    outgoing = jnp.take(tokens, cell_token, axis=0, mode="fill", fill_value=0).reshape(
        experts, capacity, model_width
    )
    arrived = lax.all_to_all(outgoing, "expert", split_axis=0, concat_axis=0, tiled=True)
    incoming = arrived.reshape(-1, model_width)
    hidden = activate(
        incoming,
        lax.all_gather(gate_proj, "dp", axis=1, tiled=True)[0],
        lax.all_gather(up_proj, "dp", axis=1, tiled=True)[0],
    )
    summed = jnp.dot(
        hidden,
        lax.all_gather(down_proj, "dp", axis=1, tiled=True)[0],
        preferred_element_type=jnp.float32,
    )
    produced = summed.astype(jnp.bfloat16).reshape(arrived.shape)
    returned = lax.all_to_all(produced, "expert", split_axis=0, concat_axis=0, tiled=True).reshape(
        -1, model_width
    )
    picked = jnp.take(returned, slot_cells, axis=0, mode="fill", fill_value=0).reshape(
        tok_dev, top_count, model_width
    )
    mixing = jnp.where(retained, route_gates, 0.0)
    branch = jnp.einsum("tk,tkd->td", mixing, picked.astype(jnp.float32))
    teacher = (tokens.astype(jnp.float32) + branch).astype(jnp.bfloat16)
    gathered = lax.all_gather(teacher, "dp", axis=0, tiled=True)
    shard_column = image_shard.reshape(-1)
    images_col = shard_column.shape[0]
    arrangement = jnp.argsort(shard_column * images_col + jnp.arange(images_col, dtype=jnp.int32))
    images = gathered.reshape(images_col, IMG_TOK, model_width)
    position = lax.axis_index("dp")
    ordered = jnp.take(images, arrangement, axis=0).reshape(images_col * IMG_TOK, model_width)
    student_rows = lax.dynamic_slice_in_dim(ordered, position * tok_dev, tok_dev, 0)
    normed = normalize(ordered, norm_gain)
    columns = lax.dynamic_slice_in_dim(normed, position * key_proj.shape[0], key_proj.shape[0], 1)
    projected = lax.psum_scatter(
        jnp.dot(columns, key_proj, preferred_element_type=jnp.float32),
        "dp",
        scatter_dimension=0,
        tiled=True,
    )
    return (student_rows, projected.astype(jnp.bfloat16))


def solution(mesh):
    in_specs = (
        P(("dp", "expert"), None),
        P("expert", "dp", None),
        P("expert", "dp", None),
        P("expert", "dp", None),
        P(("dp", "expert"), None),
        P(("dp", "expert"), None),
        P(("dp", "expert"), None),
        P(None, "expert"),
        P(),
        P("dp", None),
    )
    out_specs = (P(("dp", "expert"), None), P(("dp", "expert"), None))
    return jax.shard_map(
        per_device, mesh=mesh, in_specs=in_specs, out_specs=out_specs, check_vma=False
    )
```

profile of v0, /device:TPU:0, one launch (start us, length us, event | category | flops | bytes accessed | tf_op | source)
XLA Modules:
  0.0 194.2 jit_solution(12305694793071353915)
XLA Ops:
  0.6 190.5 %shard_map.113 = (bf16[128,4096]{1,0:T(8,128)(2,1)}, bf16[128,1024]{1,0:T(8,128)(2,1)}) custom-call(s32[2,128]{1,0:T(2,128)} %bitcast.6, s32[2,128]{1,0:T(2,128)} %bitcast.7, f32[2,128]{1,0:T(2,128)} %bitcast.8, s32[4]{0:T(128)} %bitcast.9, f32[1,4096]{1,0:T(1,128)} %bitcast.5, bf16[128,4096]{1,0:T(8,128)(2,1)} %tokens_ref.1, ...), custom_call_target="tpu_custom_call" | custom-call | tf_op jit(solution)/shard_map/pallas_call | solution.py:492
  191.2 0.0 copy-start
  191.2 2.3 %copy.14 = bf16[128,4096]{1,0:T(8,128)(2,1)} copy(bf16[128,4096]{1,0:T(8,128)(2,1)} %get-tuple-element.4) | data formatting | bytes 2097152
  193.5 0.0 copy-done
  193.5 0.7 copy.15
Async XLA Ops:
  191.2 2.3 %copy-start = (bf16[128,1024]{1,0:T(8,128)(2,1)S(1)}, bf16[128,1024]{1,0:T(8,128)(2,1)}, u32[]{:S(2)}) copy-start(bf16[128,1024]{1,0:T(8,128)(2,1)} %get-tuple-element.5) | copy-start | bytes 786436
where the time goes:
time: 197 us; the launch traced here: 194 us
  Pallas kernels  191 us (97%)
  local copies, waits for them, and re-layouts  3.04 us (2%)
    pallas_call x1, Pallas kernels, fused(): pl.pallas_call(functools.partial(fused_kernel, n_expert, capacity), out_s...  191 us

commit v1 on v0

--- a/solution.py
+++ b/solution.py
@@ -24,7 +24,9 @@
 
 
 CHUNKS = 4
-PIECES = 2
+ORDER = (
+    "G", "w0", "w1", "|", "F0", "W", "t0", "t1", "A0", "O0", "O1", "F1", "C0", "P00", "F2", "P01", "A1", "C1", "P13", "P10", "A2", "T", "K", "C2", "L1",
+)
 GROUP = 16
 MESH = pl.DeviceIdType.MESH
 
@@ -59,6 +61,10 @@
     hidden,
     gained,
     mixing,
+    far_ids,
+    far_slots,
+    far_gates,
+    key_part,
     acc_keys,
     acc_gate,
     acc_up,
@@ -85,16 +91,14 @@
     chunk = half // CHUNKS
     per_quarter = CHUNKS // 2
     key_rows, key_width = key_ref.shape
-    key_half = key_rows // 2
-    piece = key_half // PIECES
-    half_piece = piece // 2
+    key_piece = key_rows // 4
     slots = n_expert * capacity
     groups = capacity // GROUP
     block = n_expert * GROUP
     counts = {"remote": 0, "local": 0}
     sent = []
 
-    def send(source, target, where):
+    def send(source, target, where, go=True):
         index = counts["remote"]
         counts["remote"] += 1
         copy = pltpu.make_async_remote_copy(
@@ -105,7 +109,8 @@
             device_id=where,
             device_id_type=MESH,
         )
-        copy.start()
+        if go:
+            copy.start()
         sent.append(copy)
         return copy
 
@@ -145,40 +150,33 @@
     barrier = pltpu.get_barrier_semaphore()
     for where in [to_x, to_y, to_d] + [{"expert": peers[k]} for k in hops]:
         pl.semaphore_signal(barrier, inc=1, device_id=where, device_id_type=MESH)
-    pl.semaphore_wait(barrier, n_expert + 2)
-
-    mine = unit_rows(d)
-    gate_w = send(gate_ref.at[0], gate_buf.at[mine, :], to_w)
-    up_w = send(up_ref.at[0], up_buf.at[mine, :], to_w)
-    down_x, down_y, down_f, own_down = [], [], [], []
-    for p in range(2):
-        cols = pl.ds(p * quarter_width, quarter_width)
-        down_y.append(
-            send(down_ref.at[0, :, quarter_cols(dy, p)], down_buf.at[1 - core, mine, cols], to_y)
-        )
-    own_gate = local(gate_ref.at[0], gate_buf.at[mine, :])
-    own_up = local(up_ref.at[0], up_buf.at[mine, :])
-    for p in range(2):
-        cols = pl.ds(p * quarter_width, quarter_width)
-        down_x.append(send(down_ref.at[0, :, quarter_cols(d, p)], down_buf.at[core, mine, cols], to_x))
-        own_down.append(local(down_ref.at[0, :, quarter_cols(d, p)], down_buf.at[0, mine, cols]))
-    own_key = local(key_ref, key_buf.at[d])
 
     step = 512
-    grid = lax.broadcasted_iota(jnp.int32, (slots, tok_dev), 0)
-    mix = jnp.zeros((slots, tok_dev), jnp.float32)
+
+    def routes(ids, queues):
+        grid = lax.broadcasted_iota(jnp.int32, (slots, tok_dev), 0)
+        hits = []
+        for k in range(ids.shape[0]):
+            queue = queues[k : k + 1, :]
+            place = lax.div(queue, GROUP) * block + ids[k : k + 1, :] * GROUP + lax.rem(queue, GROUP)
+            hits.append(grid == jnp.where(queue < capacity, place, slots))
+        return hits
+
+    def mix_into(s, ids, queues, weights):
+        mix = jnp.zeros((slots, tok_dev), jnp.float32)
+        for k, hit in enumerate(routes(ids, queues)):
+            mix += jnp.where(hit, weights[k : k + 1, :], 0.0)
+        turned = mix.T
+        mix_hi = turned.astype(jnp.bfloat16)
+        mixing[s, 0] = mix_hi
+        mixing[s, 1] = (turned - mix_hi.astype(jnp.float32)).astype(jnp.bfloat16)
+
     named = jnp.zeros((slots, tok_dev), jnp.float32)
-    for k in range(ids_ref.shape[0]):
-        queue = slots_ref[k : k + 1, :]
-        place = lax.div(queue, GROUP) * block + ids_ref[k : k + 1, :] * GROUP + lax.rem(queue, GROUP)
-        cell = jnp.where(queue < capacity, place, slots)
-        hit = grid == cell
-        mix += jnp.where(hit, gates_ref[k : k + 1, :], 0.0)
+    for hit in routes(ids_ref, slots_ref):
         named += jnp.where(hit, 1.0, 0.0)
     spread = named.astype(jnp.bfloat16)
 
-    dispatched, forwarded = [], []
-    for g in range(groups):
+    def fill_group(g):
         chosen = spread[g * block : (g + 1) * block, :]
 
         def fill(i, carry):
@@ -188,6 +186,80 @@
             return carry
 
         lax.fori_loop(0, width // step, fill, 0)
+
+    fill_group(0)
+    pl.semaphore_wait(barrier, n_expert + 2)
+
+    mine = unit_rows(d)
+    down_x, down_y, down_f, own_down = [], [], [], []
+
+    def half_cols(p):
+        return pl.ds(p * quarter_width, quarter_width)
+
+    for p in range(2):
+        part = down_ref.at[0, :, quarter_cols(dy, p)]
+        down_y.append(send(part, down_buf.at[1 - core, mine, half_cols(p)], to_y, False))
+        part = down_ref.at[0, :, quarter_cols(d, p)]
+        down_x.append(send(part, down_buf.at[core, mine, half_cols(p)], to_x, False))
+
+    def down_to_y(p):
+        down_y[p].start()
+
+    def down_to_x(p):
+        down_x[p].start()
+
+    def down_to_w(p):
+        @pl.when(core == 0)
+        def _():
+            down_x[p].start()
+
+        @pl.when(core == 1)
+        def _():
+            down_y[p].start()
+
+    def down_to_t(p):
+        @pl.when(core == 0)
+        def _():
+            down_y[p].start()
+
+        @pl.when(core == 1)
+        def _():
+            down_x[p].start()
+
+    def down_on(p):
+        down_y[p].wait_recv()
+        part = down_buf.at[1 - core, unit_rows(dy), half_cols(p)]
+        down_f.append(send(part, down_buf.at[1, unit_rows(dy), half_cols(p)], to_x))
+
+    def down_here(p):
+        own_down[p].wait()
+        down_x[p].wait_recv()
+        down_f[p].wait_recv()
+
+    pulled = []
+
+    def pull():
+        pulled.append(send(gate_ref.at[0], gate_buf.at[mine, :], to_w))
+        pulled.append(send(up_ref.at[0], up_buf.at[mine, :], to_w))
+
+    def pulled_in():
+        own_gate.wait()
+        own_up.wait()
+        for copy in pulled:
+            copy.wait_recv()
+
+    own_gate = local(gate_ref.at[0], gate_buf.at[mine, :])
+    own_up = local(up_ref.at[0], up_buf.at[mine, :])
+    for p in range(2):
+        own_down.append(local(down_ref.at[0, :, quarter_cols(d, p)], down_buf.at[0, mine, half_cols(p)]))
+    own_key = local(key_ref, key_buf.at[d % 2])
+
+    for token in ORDER[: ORDER.index("|")]:
+        {"G": pull, "Y": down_to_y, "X": down_to_x, "w": down_to_w, "t": down_to_t}[token[0]](*[int(i) for i in token[1:]])
+    dispatched, forwarded = [], []
+    for g in range(groups):
+        if g:
+            fill_group(g)
         dispatched.append(
             {
                 k: send(
@@ -203,10 +275,7 @@
         )
         incoming[incoming_rows(g, 0, e), :] = outgoing[group_rows(g, e), :]
 
-    turned = mix.T
-    mix_hi = turned.astype(jnp.bfloat16)
-    mixing[0, 0] = mix_hi
-    mixing[0, 1] = (turned - mix_hi.astype(jnp.float32)).astype(jnp.bfloat16)
+    mix_into(0, ids_ref, slots_ref, gates_ref)
 
     def forward(g):
         for k in hops:
@@ -269,13 +338,15 @@
 
     hands = []
 
-    def give(g, cols):
-        for s in range(2):
-            returned[s, group_rows(g, e), cols] = produced[g * 2 + s, pl.ds(pl.multiple_of(e * GROUP, GROUP), GROUP), cols]
+    def give(g, count, cols):
+        span = pl.ds(2 * g, 2 * count)
+        here = pl.ds(pl.multiple_of(e * GROUP, GROUP), GROUP)
+        for i in range(2 * g, 2 * (g + count)):
+            returned[i, here, cols] = produced[i, here, cols]
         return [
             send(
-                produced.at[pl.ds(g * 2, 2), pl.ds(pl.multiple_of(peers[k] * GROUP, GROUP), GROUP), cols],
-                returned.at[:, group_rows(g, e), cols],
+                produced.at[span, pl.ds(pl.multiple_of(peers[k] * GROUP, GROUP), GROUP), cols],
+                returned.at[span, here, cols],
                 {"expert": peers[k]},
             )
             for k in hops
@@ -297,42 +368,29 @@
 
         lax.fori_loop(first, first + count, one, 0)
 
-    def key_rows_at(owner, p, start=0, size=piece):
-        first = (owner % 2) * key_half + p * piece + start
-        return pl.ds(pl.multiple_of(first, half_piece), size)
-
-    key_first, key_second, key_shared = [], [], []
-
-    def key_own(p):
-        rows = key_rows_at(e, p)
-        part = key_ref.at[rows, :]
-        place = key_buf.at[d, rows, :]
-        key_first.append((send(part, place, to_x), send(part, place, to_y)))
-
-    def pass_key(owner, rows, where):
-        part = key_buf.at[owner, rows, :]
-        return send(part, part, where)
-
-    def key_share(owner, rows):
-        key_shared.append(pass_key(owner, rows, to_sibling))
-
-    def key_middle(p):
-        key_x, key_y = key_first[p]
-        rows = key_rows_at(e, p)
-        key_y.wait_recv()
-        d0 = pass_key(dy, key_rows_at(e, p, 0, half_piece), to_x)
-        key_x.wait_recv()
-        d1 = pass_key(dx, key_rows_at(e, p, half_piece, half_piece), to_y)
-        key_second.append((d0, d1))
-        key_share(dy, rows)
-        key_share(dx, rows)
-
-    def key_diagonal(p):
-        d0, d1 = key_second[p]
-        d0.wait_recv()
-        key_share(dd, key_rows_at(e, p, 0, half_piece))
-        d1.wait_recv()
-        key_share(dd, key_rows_at(e, p, half_piece, half_piece))
+    beyond = e + 2 - 4 * ((e // 2) % 2)
+
+    def key_rows_of(who):
+        return pl.ds(pl.multiple_of((who % 4) * key_piece, key_piece), key_piece)
+
+    key_copies = []
+
+    def key_own():
+        rows = key_rows_of(e)
+        key_copies.append(send(key_ref.at[rows, :], key_buf.at[d % 2, rows, :], to_x))
+
+    def key_pass(who, where):
+        part = key_buf.at[dx % 2, key_rows_of(who), :]
+        key_copies.append(send(part, part, where))
+
+    def key_share():
+        key_copies[0].wait_recv()
+        key_pass(e, {"expert": beyond})
+        key_pass(e, to_sibling)
+
+    def key_relay():
+        key_copies[1].wait_recv()
+        key_pass(beyond, to_sibling)
 
     def collect(g):
         for copy in handed[g]:
@@ -345,17 +403,17 @@
     acc_keys[...] = jnp.zeros_like(acc_keys)
     squares[...] = jnp.zeros_like(squares)
     owners = (d, dy, dx, dd)
-    tile_w, tile_t = [], []
+    tile_w, tile_t, key_sums = [], [], []
 
     def flag(owner, shard):
         return jnp.where(shard_ref[owner] == shard, 1.0, 0.0)
 
     def combine(c):
-        for copy in hands[groups - 1 + c]:
+        for copy in hands[c]:
             copy.wait_recv()
         cols = pl.ds(c * chunk, chunk)
         for s in range(2):
-            rows = returned[s, :, cols]
+            rows = jnp.concatenate([returned[2 * g + s, :, cols] for g in range(groups)], axis=0)
             branch = jnp.dot(mixing[s, 0], rows, preferred_element_type=jnp.float32)
             branch += jnp.dot(mixing[s, 1], rows, preferred_element_type=jnp.float32)
             base = tokens_ref[:, chunk_cols(d, c)] if s == 0 else tok_half[:, cols]
@@ -364,7 +422,6 @@
 
     def keep(rows, at):
         student_ref[:, at] = rows.astype(jnp.bfloat16)
-        gained[:, at] = (rows * gain_ref[:, at]).astype(jnp.bfloat16)
         squares[...] += jnp.sum(rows * rows, axis=-1, keepdims=True)
 
     def swap(c):
@@ -378,83 +435,103 @@
             leave += flag(owners[slot], dy) * rows
         passed[:, cols] = leave.astype(jnp.bfloat16)
         tile_t.append(send(passed.at[:, cols], far.at[:, cols], to_y))
-        keep(stay, chunk_cols(d, c))
+        at = chunk_cols(d, c)
+        gain = gain_ref[:, at]
+        gained[:tok_dev, cols] = (stay * gain).astype(jnp.bfloat16)
+        gained[tok_dev:, cols] = (leave * gain).astype(jnp.bfloat16)
+        keep(stay, at)
 
     def finish(c):
         tile_t[c].wait_recv()
         keep(far[:, pl.ds(c * chunk, chunk)].astype(jnp.float32), chunk_cols(dy, c))
 
-    def keys_of(owner, c):
-        q = quarter_of(owner, c // per_quarter)
+    def keys_of(c):
         acc_keys[...] += jnp.dot(
-            gained[:, chunk_cols(owner, c)],
-            key_buf[q, pl.ds((c % per_quarter) * chunk, chunk), :],
+            gained[:, pl.ds(c * chunk, chunk)],
+            key_buf[c // per_quarter, pl.ds((c % per_quarter) * chunk, chunk), :],
             preferred_element_type=jnp.float32,
         )
 
-    forward(0)
-    for p in range(2):
-        cols = pl.ds(p * quarter_width, quarter_width)
-        down_y[p].wait_recv()
-        part = down_buf.at[1 - core, unit_rows(dy), cols]
-        down_f.append(send(part, down_buf.at[1, unit_rows(dy), cols], to_x))
-    forward(1)
-    for copy in (own_gate, own_up):
-        copy.wait()
-    for copy in (gate_w, up_w):
-        copy.wait_recv()
-    activate(0)
-    for g in range(1, groups - 1):
-        activate(g)
-    for g in range(2, groups):
-        forward(g)
-    others = [send(mixing.at[0], mixing.at[1], to_y)]
-    for p in range(2):
-        cols = pl.ds(p * quarter_width, quarter_width)
-        others.append(send(tokens_ref.at[:, quarter_cols(dy, p)], tok_half.at[:, cols], to_y))
-    for copy in own_down:
-        copy.wait()
-    for copy in down_x + down_f:
-        copy.wait_recv()
-    every = pl.ds(0, half)
-    for g in range(groups):
-        if g == 1:
-            activate(groups - 1)
-            for p in range(PIECES):
-                key_own(p)
-        collect(g)
-        if g < groups - 1:
+    early, others = [], []
+
+    def push(g, p):
+        if g == 0:
+            down_here(p)
+        elif p == 3:
             project(g, 0, CHUNKS)
-            hands.append(give(g, every))
-        else:
-            for c in range(CHUNKS):
-                project(g, c, 1)
-                hands.append(give(g, pl.ds(c * chunk, chunk)))
-    for p in range(PIECES):
-        key_middle(p)
-    for p in range(PIECES):
-        key_diagonal(p)
+            return
+        elif p == 2:
+            project(g, 0, CHUNKS)
+            early.extend(give(g, 1, pl.ds(0, half)))
+            return
+        project(g, p * per_quarter, per_quarter)
+        if p < 3:
+            early.extend(give(g, 1, half_cols(p)))
+
+    def last(p):
+        for c in range(CHUNKS):
+            project(groups - 1, c, 1)
+            first = 1 if c >= p * per_quarter else groups - 1
+            hands.append(give(first, groups - first, pl.ds(c * chunk, chunk)))
+
+    def spread_rest():
+        for ref, there in ((ids_ref, far_ids), (slots_ref, far_slots), (gates_ref, far_gates)):
+            others.append(send(ref, there, to_y))
+        for p in range(2):
+            others.append(send(tokens_ref.at[:, quarter_cols(dy, p)], tok_half.at[:, half_cols(p)], to_y))
+
+    table = {
+        "Y": down_to_y,
+        "X": down_to_x,
+        "w": down_to_w,
+        "t": down_to_t,
+        "O": down_on,
+        "F": forward,
+        "W": pulled_in,
+        "A": activate,
+        "C": collect,
+        "P": push,
+        "L": last,
+        "T": spread_rest,
+        "K": key_own,
+        "S": key_share,
+    }
+    for token in ORDER[ORDER.index("|") + 1 :]:
+        table[token[0]](*[int(i) for i in token[1:]])
     for copy in others:
         copy.wait_recv()
-    for g in range(groups - 1):
-        for copy in hands[g]:
-            copy.wait_recv()
+    mix_into(1, far_ids, far_slots, far_gates)
+    if len(key_copies) == 1:
+        key_share()
+    for copy in early:
+        copy.wait_recv()
     own_key.wait()
     for c in range(CHUNKS + 2):
         if c < CHUNKS:
             combine(c)
+        if c == CHUNKS:
+            key_relay()
+            for copy in key_copies[2:]:
+                copy.wait_recv()
+            for i in range(CHUNKS - 1):
+                keys_of(i)
         if 0 <= c - 1 < CHUNKS:
             swap(c - 1)
-        if c == 1:
-            for copy in key_shared:
-                copy.wait_recv()
-        if 0 <= c - 1 < CHUNKS:
-            keys_of(d, c - 1)
-        if 0 <= c - 2 < CHUNKS:
+        if 0 <= c - 2 < CHUNKS - 1:
             finish(c - 2)
-            keys_of(dy, c - 2)
+    keys_of(CHUNKS - 1)
+    part_width = key_width // 2
+    for n in range(2):
+        cols = pl.ds(n * part_width, part_width)
+        key_part[0, :, cols] = acc_keys[tok_dev:, cols].astype(jnp.bfloat16)
+        key_sums.append(send(key_part.at[0, :, cols], key_part.at[1, :, cols], to_y))
+    finish(CHUNKS - 1)
     scale = lax.rsqrt(squares[...] / width + 1e-05)
-    keys_ref[...] = (acc_keys[...] * scale).astype(jnp.bfloat16)
+    for n in range(2):
+        cols = pl.ds(n * part_width, part_width)
+        key_sums[n].wait_recv()
+        total = acc_keys[:tok_dev, cols] + key_part[1, :, cols].astype(jnp.float32)
+        keys_ref[:, cols] = (total * scale).astype(jnp.bfloat16)
     for copy in sent:
         copy.wait_send()
 
@@ -484,7 +561,7 @@
     units = gate_proj.shape[1]
     half_width = width // 2
     key_rows, key_width = key_proj.shape
-    remote = 8 + 8 * PIECES + (n_expert - 1) * (2 * groups + groups - 1 + CHUNKS) + 3 * groups + 3 + 2 * CHUNKS
+    remote = 14 + (n_expert - 1) * (4 * groups + CHUNKS) + 3 * groups + 5 + 2 * CHUNKS
     vmem = pl.BlockSpec(memory_space=pltpu.VMEM)
     anywhere = pl.BlockSpec(memory_space=pl.ANY)
     scalars = pl.BlockSpec(memory_space=pltpu.SMEM)
@@ -501,19 +578,23 @@
             pltpu.VMEM((2 * units, width), half),
             pltpu.VMEM((2 * units, width), half),
             pltpu.VMEM((2, 2 * units, half_width), half),
-            pltpu.VMEM((4, key_rows, key_width), half),
+            pltpu.VMEM((2, key_rows, key_width), half),
             pltpu.VMEM((slots, width), half),
             pltpu.VMEM((2 * slots, width), half),
             pltpu.VMEM((2 * groups, n_expert * GROUP, half_width), half),
-            pltpu.VMEM((2, slots, half_width), half),
+            pltpu.VMEM((2 * groups, n_expert * GROUP, half_width), half),
             pltpu.VMEM((4, tok_dev, half_width), half),
             pltpu.VMEM((tok_dev, half_width), half),
             pltpu.VMEM((tok_dev, half_width), half),
             pltpu.VMEM((tok_dev, half_width), half),
             pltpu.VMEM((5, slots, 2 * units), half),
-            pltpu.VMEM((tok_dev, width), half),
+            pltpu.VMEM((2 * tok_dev, half_width), half),
             pltpu.VMEM((2, 2, tok_dev, slots), half),
-            pltpu.VMEM((tok_dev, key_width), jnp.float32),
+            pltpu.VMEM((route_ids.shape[1], tok_dev), jnp.int32),
+            pltpu.VMEM((route_ids.shape[1], tok_dev), jnp.int32),
+            pltpu.VMEM((route_ids.shape[1], tok_dev), jnp.float32),
+            pltpu.VMEM((2, tok_dev, key_width), half),
+            pltpu.VMEM((2 * tok_dev, key_width), jnp.float32),
             pltpu.VMEM((2 * n_expert * GROUP, 2 * units), jnp.float32),
             pltpu.VMEM((2 * n_expert * GROUP, 2 * units), jnp.float32),
             pltpu.VMEM((tok_dev, 1), jnp.float32),
@@ -556,7 +637,7 @@
     top_count = route_ids.shape[1]
     experts = gate_proj.shape[0] * lax.axis_size("expert")
     capacity = 3 * tok_dev * top_count // (2 * experts)
-    if capacity % 16 == 0 and gate_proj.shape[0] == 1 and lax.axis_size("dp") == 4 and experts % 2 == 0:
+    if capacity % 16 == 0 and gate_proj.shape[0] == 1 and lax.axis_size("dp") == 4 and experts % 4 == 0 and capacity >= 32:
         if tok_dev == IMG_TOK and gate_proj.shape[1] % 64 == 0 and key_proj.shape[0] % 512 == 0:
             return fused(
                 tokens,

time: 197 us -> 180 us (0.914); the launches traced: 194 us -> 179 us
  Pallas kernels: 191 us -> 176 us
    pallas_call x1, Pallas kernels: 191 us -> 176 us  [fused(): pl.pallas_call(functools.partial(fused_kernel, n_expert, capacity), out_s...]
where the time goes in v1:
time: 180 us; the launch traced here: 179 us
  Pallas kernels  176 us (98%)
  local copies, waits for them, and re-layouts  3.04 us (2%)
    pallas_call x1, Pallas kernels, fused(): pl.pallas_call(functools.partial(fused_kernel, n_expert, capacity), out_s...  176 us

profile of v1, /device:TPU:0, one launch (start us, length us, event | category | flops | bytes accessed | tf_op | source)
XLA Modules:
  0.0 179.5 jit_solution(13931490355871007169)
XLA Ops:
  0.6 175.8 %shard_map.113 = (bf16[128,4096]{1,0:T(8,128)(2,1)}, bf16[128,1024]{1,0:T(8,128)(2,1)}) custom-call(s32[2,128]{1,0:T(2,128)} %bitcast.6, s32[2,128]{1,0:T(2,128)} %bitcast.7, f32[2,128]{1,0:T(2,128)} %bitcast.8, s32[4]{0:T(128)} %bitcast.9, f32[1,4096]{1,0:T(1,128)} %bitcast.5, bf16[128,4096]{1,0:T(8,128)(2,1)} %tokens_ref.1, ...), custom_call_target="tpu_custom_call" | custom-call | tf_op jit(solution)/shard_map/pallas_call | solution.py:569
  176.4 0.0 copy-start
  176.4 2.3 %copy.14 = bf16[128,4096]{1,0:T(8,128)(2,1)} copy(bf16[128,4096]{1,0:T(8,128)(2,1)} %get-tuple-element.4) | data formatting | bytes 2097152
  178.7 0.0 copy-done
  178.8 0.7 copy.15
Async XLA Ops:
  176.4 2.3 %copy-start = (bf16[128,1024]{1,0:T(8,128)(2,1)S(1)}, bf16[128,1024]{1,0:T(8,128)(2,1)}, u32[]{:S(2)}) copy-start(bf16[128,1024]{1,0:T(8,128)(2,1)} %get-tuple-element.5) | copy-start | bytes 786436

commit v2 on v1

--- a/solution.py
+++ b/solution.py
@@ -24,8 +24,9 @@
 
 
 CHUNKS = 4
+SHARE_AT = 1
 ORDER = (
-    "G", "w0", "w1", "|", "F0", "W", "t0", "t1", "A0", "O0", "O1", "F1", "C0", "P00", "F2", "P01", "A1", "C1", "P13", "P10", "A2", "T", "K", "C2", "L1",
+    "G", "w0", "w1", "|", "F0", "W", "t0", "t1", "A0", "O0", "O1", "F1", "C0", "P00", "F2", "P01", "A1", "C1", "P13", "P10", "A2", "T0", "T1", "K", "C2", "L0", "L1", "S",
 )
 GROUP = 16
 MESH = pl.DeviceIdType.MESH
@@ -65,6 +66,8 @@
     far_slots,
     far_gates,
     key_part,
+    student,
+    keys,
     acc_keys,
     acc_gate,
     acc_up,
@@ -122,8 +125,8 @@
         return copy
 
     to_x, to_y, to_sibling = {"dp": dx}, {"dp": dy}, {"expert": sibling}
-    to_w, to_t, to_d = {"dp": w}, {"dp": t}, {"dp": dd}
-    hops = range(1, n_expert)
+    to_w, to_t = {"dp": w}, {"dp": t}
+    hops = sorted(range(1, n_expert), key=lambda k: -min(k, n_expert - k))
     peers = {k: lax.rem(e + k, n_expert) for k in hops}
     senders = {k: lax.rem(e + n_expert - k, n_expert) for k in hops}
 
@@ -148,7 +151,7 @@
         return pl.ds(pl.multiple_of((g * 2 + s) * block + who * GROUP, GROUP), GROUP)
 
     barrier = pltpu.get_barrier_semaphore()
-    for where in [to_x, to_y, to_d] + [{"expert": peers[k]} for k in hops]:
+    for where in [to_x, to_y, {"dp": dd}] + [{"expert": peers[k]} for k in hops]:
         pl.semaphore_signal(barrier, inc=1, device_id=where, device_id_type=MESH)
 
     step = 512
@@ -327,7 +330,7 @@
             dst_ref=hidden.at[3, at, :],
             send_sem=spare_send.at[g],
             recv_sem=spare_recv.at[g],
-            device_id=to_d,
+            device_id={"dp": dd},
             device_id_type=MESH,
         )
         spares.append(spare)
@@ -420,8 +423,11 @@
             tiles[s, :, cols] = (base.astype(jnp.float32) + branch).astype(jnp.bfloat16)
         tile_w.append(send(tiles.at[pl.ds(0, 2), :, cols], tiles.at[pl.ds(2, 2), :, cols], to_x))
 
+    written = []
+
     def keep(rows, at):
-        student_ref[:, at] = rows.astype(jnp.bfloat16)
+        student[:, at] = rows.astype(jnp.bfloat16)
+        written.append(local(student.at[:, at], student_ref.at[:, at]))
         squares[...] += jnp.sum(rows * rows, axis=-1, keepdims=True)
 
     def swap(c):
@@ -469,16 +475,27 @@
             early.extend(give(g, 1, half_cols(p)))
 
     def last(p):
-        for c in range(CHUNKS):
+        for c in range(p * per_quarter, (p + 1) * per_quarter):
             project(groups - 1, c, 1)
-            first = 1 if c >= p * per_quarter else groups - 1
+            first = 1 if p else groups - 1
             hands.append(give(first, groups - first, pl.ds(c * chunk, chunk)))
 
-    def spread_rest():
-        for ref, there in ((ids_ref, far_ids), (slots_ref, far_slots), (gates_ref, far_gates)):
-            others.append(send(ref, there, to_y))
-        for p in range(2):
-            others.append(send(tokens_ref.at[:, quarter_cols(dy, p)], tok_half.at[:, half_cols(p)], to_y))
+    def early_in():
+        for copy in early:
+            copy.wait_recv()
+        early.clear()
+
+    for ref, there in ((ids_ref, far_ids), (slots_ref, far_slots), (gates_ref, far_gates)):
+        others.append(send(ref, there, to_y, False))
+    for p in range(2):
+        part = tokens_ref.at[:, quarter_cols(dy, p)]
+        others.append(send(part, tok_half.at[:, half_cols(p)], to_y, False))
+
+    def spread_rest(which):
+        @pl.when(core == which)
+        def _():
+            for copy in others:
+                copy.start()
 
     table = {
         "Y": down_to_y,
@@ -492,6 +509,7 @@
         "C": collect,
         "P": push,
         "L": last,
+        "E": early_in,
         "T": spread_rest,
         "K": key_own,
         "S": key_share,
@@ -501,10 +519,9 @@
     for copy in others:
         copy.wait_recv()
     mix_into(1, far_ids, far_slots, far_gates)
-    if len(key_copies) == 1:
-        key_share()
-    for copy in early:
-        copy.wait_recv()
+    if not key_copies:
+        key_own()
+    early_in()
     own_key.wait()
     for c in range(CHUNKS + 2):
         if c < CHUNKS:
@@ -515,6 +532,8 @@
                 copy.wait_recv()
             for i in range(CHUNKS - 1):
                 keys_of(i)
+        if c == SHARE_AT and len(key_copies) == 1:
+            key_share()
         if 0 <= c - 1 < CHUNKS:
             swap(c - 1)
         if 0 <= c - 2 < CHUNKS - 1:
@@ -526,19 +545,25 @@
         key_part[0, :, cols] = acc_keys[tok_dev:, cols].astype(jnp.bfloat16)
         key_sums.append(send(key_part.at[0, :, cols], key_part.at[1, :, cols], to_y))
     finish(CHUNKS - 1)
+    for copy in sent[:-2]:
+        copy.wait_send()
+
+    @pl.when(core == 1)
+    def _():
+        for copy in spares:
+            copy.wait_send()
+
     scale = lax.rsqrt(squares[...] / width + 1e-05)
     for n in range(2):
         cols = pl.ds(n * part_width, part_width)
         key_sums[n].wait_recv()
         total = acc_keys[:tok_dev, cols] + key_part[1, :, cols].astype(jnp.float32)
-        keys_ref[:, cols] = (total * scale).astype(jnp.bfloat16)
-    for copy in sent:
+        keys[:, cols] = (total * scale).astype(jnp.bfloat16)
+        written.append(local(keys.at[:, cols], keys_ref.at[:, cols]))
+    for copy in sent[-2:]:
         copy.wait_send()
-
-    @pl.when(core == 1)
-    def _():
-        for copy in spares:
-            copy.wait_send()
+    for copy in written:
+        copy.wait()
 
 
 def fused(
@@ -573,7 +598,7 @@
             jax.ShapeDtypeStruct((tok_dev, key_width), half),
         ),
         in_specs=[vmem] * 3 + [scalars] + [vmem] * 2 + [anywhere] * 4,
-        out_specs=(vmem, vmem),
+        out_specs=(anywhere, anywhere),
         scratch_shapes=[
             pltpu.VMEM((2 * units, width), half),
             pltpu.VMEM((2 * units, width), half),
@@ -594,6 +619,8 @@
             pltpu.VMEM((route_ids.shape[1], tok_dev), jnp.int32),
             pltpu.VMEM((route_ids.shape[1], tok_dev), jnp.float32),
             pltpu.VMEM((2, tok_dev, key_width), half),
+            pltpu.VMEM((tok_dev, width), half),
+            pltpu.VMEM((tok_dev, key_width), half),
             pltpu.VMEM((2 * tok_dev, key_width), jnp.float32),
             pltpu.VMEM((2 * n_expert * GROUP, 2 * units), jnp.float32),
             pltpu.VMEM((2 * n_expert * GROUP, 2 * units), jnp.float32),
@@ -602,7 +629,7 @@
             pltpu.SemaphoreType.DMA((remote,)),
             pltpu.SemaphoreType.DMA((groups,)),
             pltpu.SemaphoreType.DMA((groups,)),
-            pltpu.SemaphoreType.DMA((5,)),
+            pltpu.SemaphoreType.DMA((5 + 2 * CHUNKS + 2,)),
         ],
         compiler_params=pltpu.CompilerParams(
             collective_id=0, has_side_effects=True, vmem_limit_bytes=60 * 1024 * 1024

time: 180 us -> 178 us (0.989)
  no operation moved by 1% of the time
where the time goes in v2:
time: 178 us
  Pallas kernels  175 us (98%)
  local copies, waits for them, and re-layouts  3.04 us (2%)
    pallas_call x1, Pallas kernels, fused(): pl.pallas_call(functools.partial(fused_kernel, n_expert, capacity), out_s...  175 us

profile of v2, /device:TPU:0, one launch (start us, length us, event | category | flops | bytes accessed | tf_op | source)
XLA Modules:
  0.0 178.3 jit_solution(7329292039408728075)
XLA Ops:
  0.6 174.6 %shard_map.113 = (bf16[128,4096]{1,0:T(8,128)(2,1)}, bf16[128,1024]{1,0:T(8,128)(2,1)}) custom-call(s32[2,128]{1,0:T(2,128)} %bitcast.6, s32[2,128]{1,0:T(2,128)} %bitcast.7, f32[2,128]{1,0:T(2,128)} %bitcast.8, s32[4]{0:T(128)} %bitcast.9, f32[1,4096]{1,0:T(1,128)} %bitcast.5, bf16[128,4096]{1,0:T(8,128)(2,1)} %tokens_ref.1, ...), custom_call_target="tpu_custom_call" | custom-call | tf_op jit(solution)/shard_map/pallas_call | solution.py:594
  175.2 0.0 copy-start
  175.2 2.3 %copy.14 = bf16[128,4096]{1,0:T(8,128)(2,1)} copy(bf16[128,4096]{1,0:T(8,128)(2,1)} %get-tuple-element.4) | data formatting | bytes 2097152
  177.6 0.0 copy-done
  177.6 0.7 copy.15
Async XLA Ops:
  175.2 2.3 %copy-start = (bf16[128,1024]{1,0:T(8,128)(2,1)S(1)}, bf16[128,1024]{1,0:T(8,128)(2,1)}, u32[]{:S(2)}) copy-start(bf16[128,1024]{1,0:T(8,128)(2,1)} %get-tuple-element.5) | copy-start | bytes 786436
